TPU v7x, 32 devices: a whole 2x2x4 slice. The times are simulated.
32 devices in a mesh: tp: 4 (over z), dp: 8 (over y, x, core).
Axes of the slice: x: 2, y: 2, z: 4, core: 2. Of those that a mesh axis runs over, the one named last changes fastest.
Arguments:
- x_in: bfloat16 [4096, 2304], P('dp')
- w_gate: bfloat16 [2304, 9216], P('dp', 'tp')
- w_up: bfloat16 [2304, 9216], P('dp', 'tp')
- w_down: bfloat16 [9216, 2304], P('tp', 'dp')
- dy_in: bfloat16 [4096, 2304], P('dp')
Outputs:
- output 1: bfloat16 [4096, 2304], P('dp')
- output 2: bfloat16 [4096, 2304], P('dp')
- output 3: float32 [2304, 9216], P('dp', 'tp')
- output 4: float32 [2304, 9216], P('dp', 'tp')
- output 5: float32 [9216, 2304], P('tp', 'dp')
All inputs are finite; a program needn't handle non-finite values.
Results may differ from a plain program's by a relative error of at most 0.001.
Values are sent between devices in bfloat16 or wider.
A program may use at most 1 GiB of HBM per device.

v0:
```python
import jax
import jax.numpy as jnp
from jax import lax
from jax.sharding import PartitionSpec as P


def solution(mesh):
    def device_pass(x_rows, gate_blk, up_blk, down_blk, dy_rows):
        x_cols = lax.all_to_all(x_rows, 'dp', 1, 0, tiled=True)
        gate_part = jnp.dot(x_cols, gate_blk, preferred_element_type=jnp.float32)
        up_part = jnp.dot(x_cols, up_blk, preferred_element_type=jnp.float32)
        gate_pre = lax.psum_scatter(gate_part, 'dp', scatter_dimension=0, tiled=True)
        up_pre = lax.psum_scatter(up_part, 'dp', scatter_dimension=0, tiled=True)
        sig_gate = jax.nn.sigmoid(gate_pre)
        silu_gate = gate_pre * sig_gate
        hidden = (silu_gate * up_pre).astype(jnp.bfloat16)
        hidden_all = lax.all_gather(hidden, 'dp', axis=0, tiled=True)
        out_part = jnp.dot(hidden_all, down_blk, preferred_element_type=jnp.float32)
        y_cols = (x_cols.astype(jnp.float32) + lax.psum(out_part, 'tp')).astype(jnp.bfloat16)
        y_rows = lax.all_to_all(y_cols, 'dp', 0, 1, tiled=True)
        dy_cols = lax.all_to_all(dy_rows, 'dp', 1, 0, tiled=True)
        grad_part = jnp.einsum('td,fd->tf', dy_cols, down_blk, preferred_element_type=jnp.float32)
        grad_h = lax.psum_scatter(grad_part, 'dp', scatter_dimension=0, tiled=True)
        d_gate = (grad_h * up_pre * sig_gate * (1.0 + gate_pre * (1.0 - sig_gate))).astype(jnp.bfloat16)
        d_up = (grad_h * silu_gate).astype(jnp.bfloat16)
        gate_all = lax.all_gather(d_gate, 'dp', axis=0, tiled=True)
        up_all = lax.all_gather(d_up, 'dp', axis=0, tiled=True)
        dx_part = (jnp.einsum('tf,df->td', gate_all, gate_blk, preferred_element_type=jnp.float32)
                   + jnp.einsum('tf,df->td', up_all, up_blk, preferred_element_type=jnp.float32))
        dx_cols = (dy_cols.astype(jnp.float32) + lax.psum(dx_part, 'tp')).astype(jnp.bfloat16)
        dx_rows = lax.all_to_all(dx_cols, 'dp', 0, 1, tiled=True)
        dw_gate = jnp.einsum('td,tf->df', x_cols, gate_all, preferred_element_type=jnp.float32)
        dw_up = jnp.einsum('td,tf->df', x_cols, up_all, preferred_element_type=jnp.float32)
        dw_down = jnp.einsum('tf,td->fd', hidden_all, dy_cols, preferred_element_type=jnp.float32)
        return y_rows, dx_rows, dw_gate, dw_up, dw_down

    row_spec = P('dp', None)
    weight_spec = P('dp', 'tp')
    down_spec = P('tp', 'dp')
    return jax.shard_map(device_pass, mesh=mesh,
                         in_specs=(row_spec, weight_spec, weight_spec, down_spec, row_spec),
                         out_specs=(row_spec, row_spec, weight_spec, weight_spec, down_spec),
                         check_vma=False)
```

profile of v0, /device:TPU:0, one launch (start us, length us, event | category | flops | bytes accessed | tf_op | source)
XLA Modules:
  0.0 1485.4 jit_solution(12927675748125469525)
XLA Ops:
  7.2 4.4 copy.17
  11.6 34.4 %all_to_all.76 = bf16[512,8,288]{0,2,1:T(8,128)(2,1)S(1)} all-to-all(bf16[512,8,288]{0,2,1:T(8,128)(2,1)} %bitcast.58), channel_id=1, replica_groups=mesh['tp'=4,'dp'=8] {'dp'}, dimensions={1} | all-to-all | bytes 4718592 | tf_op jit(solution)/shard_map/all_to_all | solution.py:21
  46.3 1.4 copy-done.4
  47.7 16.4 %fusion.4 = f32[4096,2304]{1,0:T(8,128)} fusion(bf16[4096,288]{0,1:T(8,128)(2,1)S(1)} %bitcast.49, bf16[2304,288]{0,1:T(8,128)(2,1)S(1)} %copy-done), kind=kOutput, calls=%fused_computation.15 | convolution fusion | flops 5435817984 | bytes 41435136 | tf_op jit(solution)/shard_map/td,fd->tf/dot_general | solution.py:22
  64.1 4.3 copy.14
  68.4 32.7 %all_to_all.77 = bf16[512,8,288]{0,2,1:T(8,128)(2,1)S(1)} all-to-all(bf16[512,8,288]{0,2,1:T(8,128)(2,1)} %bitcast.59), channel_id=1, replica_groups=mesh['tp'=4,'dp'=8] {'dp'}, dimensions={1} | all-to-all | bytes 4718592 | tf_op jit(solution)/shard_map/all_to_all | solution.py:9
  101.4 1.4 copy-done.2
  102.8 16.3 %fusion.2 = f32[4096,2304]{1,0:T(8,128)} fusion(bf16[4096,288]{0,1:T(8,128)(2,1)S(1)} %bitcast.44, bf16[288,2304]{1,0:T(8,128)(2,1)S(1)} %copy-done.7), kind=kOutput, calls=%fused_computation.13 | convolution fusion | flops 5435817984 | bytes 41435136 | tf_op jit(solution)/shard_map/dot_general | solution.py:11
  120.4 18.0 %fusion.1 = f32[4096,2304]{1,0:T(8,128)} fusion(bf16[4096,288]{0,1:T(8,128)(2,1)} %bitcast.45, bf16[288,2304]{1,0:T(8,128)(2,1)S(1)} %copy-done.6), kind=kOutput, calls=%fused_computation.12 | convolution fusion | flops 5435817984 | bytes 41435136 | tf_op jit(solution)/shard_map/dot_general | solution.py:10
  138.7 149.5 %reduce-scatter.8.cloned.1.call-done = f32[512,2304]{1,0:T(8,128)} async-done(((f32[4096,2304]{1,0:T(8,128)}), f32[512,2304]{1,0:T(8,128)}) %reduce-scatter.8.cloned.1.call-update) | async-done | bytes 4718608 | tf_op jit(solution)/shard_map/reduce_scatter | solution.py:23
  288.2 228.3 %reduce-scatter.6.cloned.1.call-done = f32[512,2304]{1,0:T(8,128)} async-done(((f32[4096,2304]{1,0:T(8,128)}), f32[512,2304]{1,0:T(8,128)}) %reduce-scatter.6.cloned.1.call-update) | async-done | bytes 4718608 | tf_op jit(solution)/shard_map/reduce_scatter | solution.py:13
  516.5 228.3 %reduce-scatter.4.cloned.1.call-done = f32[512,2304]{1,0:T(8,128)} async-done(((f32[4096,2304]{1,0:T(8,128)}), f32[512,2304]{1,0:T(8,128)}) %reduce-scatter.4.cloned.1.call-update) | async-done | bytes 4718608 | tf_op jit(solution)/shard_map/reduce_scatter | solution.py:12
  744.8 8.1 multiply_convert_fusion
  754.1 97.5 %all-gather.4.cloned.1.call-done = bf16[4096,2304]{1,0:T(8,128)(2,1)} async-done(((bf16[512,2304]{1,0:T(8,128)(2,1)}), bf16[4096,2304]{1,0:T(8,128)(2,1)}) %all-gather.4.cloned.1.call-update) | async-done | bytes 18874384 | tf_op jit(solution)/shard_map/all_gather | solution.py:17
  851.6 11.8 fusion.3
  863.4 89.1 %all-gather.6.cloned.1.call-done = bf16[4096,2304]{1,0:T(8,128)(2,1)} async-done(((bf16[512,2304]{1,0:T(8,128)(2,1)}), bf16[4096,2304]{1,0:T(8,128)(2,1)}) %all-gather.6.cloned.1.call-update) | async-done | bytes 18874384 | tf_op jit(solution)/shard_map/all_gather | solution.py:26
  952.5 11.8 fusion.5
  964.2 89.1 %all-gather.8.cloned.1.call-done = bf16[4096,2304]{1,0:T(8,128)(2,1)} async-done(((bf16[512,2304]{1,0:T(8,128)(2,1)}), bf16[4096,2304]{1,0:T(8,128)(2,1)}) %all-gather.8.cloned.1.call-update) | async-done | bytes 18874384 | tf_op jit(solution)/shard_map/all_gather | solution.py:27
  1053.3 21.0 %convolution_add_fusion = f32[4096,288]{0,1:T(8,128)} fusion(f32[4096,288]{0,1:T(8,128)} %fusion.5, bf16[4096,2304]{1,0:T(8,128)(2,1)} %all-gather.8.cloned.1.call-done, bf16[288,2304]{1,0:T(8,128)(2,1)S(1)} %copy-done.8), kind=kOutput, calls=%fused_computation | convolution fusion | flops 5436997632 | bytes 29638656 | tf_op jit(solution)/shard_map/tf,df->td/dot_general | solution.py:29
  1074.3 322.8 %all-reduce.3.cloned.1.call-done = (f32[4096,288]{0,1:T(8,128)}, f32[4096,288]{0,1:T(8,128)}) async-done(((f32[4096,288]{0,1:T(8,128)}, f32[4096,288]{0,1:T(8,128)}), (f32[4096,288]{0,1:T(8,128)}, f32[4096,288]{0,1:T(8,128)})) %all-reduce.3.cloned.1.call-update) | async-done | bytes 9437200 | tf_op jit(solution)/shard_map/psum | solution.py:19
  1397.1 8.1 add_convert_fusion
  1405.2 1.6 copy.29
  1406.8 4.6 all-to-all-start.1
  1411.4 13.8 fusion.6
  1425.2 1.7 copy.28
  1426.8 13.7 all-to-all-done.1
  1440.5 4.5 all-to-all-start.3
  1445.1 13.8 convolution_bitcast_fusion.1
  1458.9 7.1 convolution_bitcast_fusion
  1466.0 4.4 copy.20
  1470.4 3.9 all-to-all-done.3
  1474.3 4.3 copy.21
  (43 shorter events, 3.4 us)
Async XLA Ops:
  7.2 40.5 %copy-start = (bf16[2304,288]{0,1:T(8,128)(2,1)S(1)}, bf16[2304,288]{0,1:T(8,128)(2,1)}, u32[]{:S(2)}) copy-start(bf16[2304,288]{0,1:T(8,128)(2,1)} %param.8) | copy-start | bytes 3981316
  7.2 281.0 %reduce-scatter.8.cloned.1.call-start = ((), (), s32[]{:S(2)}) async-start(), calls=%async_computation.10 | async-start | bytes 42467328 | tf_op jit(solution)/shard_map/reduce_scatter | solution.py:23
  46.3 1.4 copy-start.4
  64.1 452.4 %reduce-scatter.6.cloned.1.call-start = ((), (), s32[]{:S(2)}) async-start(), calls=%async_computation.8 | async-start | bytes 42467328 | tf_op jit(solution)/shard_map/reduce_scatter | solution.py:13
  101.1 1.7 copy-start.7
  101.3 1.4 copy-start.2
  119.1 1.3 copy-start.6
  119.1 625.6 %reduce-scatter.4.cloned.1.call-start = ((), (), s32[]{:S(2)}) async-start(), calls=%async_computation.7 | async-start | bytes 42467328 | tf_op jit(solution)/shard_map/reduce_scatter | solution.py:12
  138.4 713.2 %all-gather.4.cloned.1.call-start = ((), (), s32[]{:S(2)}) async-start(), calls=%async_computation.9 | async-start | bytes 21233664 | tf_op jit(solution)/shard_map/all_gather | solution.py:17
  752.9 199.6 %all-gather.6.cloned.1.call-start = ((), (), s32[]{:S(2)}) async-start(), calls=%async_computation.11 | async-start | bytes 21233664 | tf_op jit(solution)/shard_map/all_gather | solution.py:26
  753.5 299.8 %all-gather.8.cloned.1.call-start = ((), (), s32[]{:S(2)}) async-start(), calls=%async_computation.12 | async-start | bytes 21233664 | tf_op jit(solution)/shard_map/all_gather | solution.py:27
  754.1 643.0 %all-reduce.3.cloned.1.call-start = ((), (), s32[]{:S(2)}) async-start(), calls=%async_computation.13 | async-start | bytes 18874368 | tf_op jit(solution)/shard_map/psum | solution.py:19
  863.4 189.9 %copy-start.8 = (bf16[288,2304]{1,0:T(8,128)(2,1)S(1)}, bf16[288,2304]{1,0:T(8,128)(2,1)}, u32[]{:S(2)}) copy-start(bf16[288,2304]{1,0:T(8,128)(2,1)} %param.7) | copy-start | bytes 3981316
  1406.8 33.7 %all-to-all-start.1 = ((bf16[8,512,288]{1,2,0:T(8,128)(2,1)}), bf16[8,512,288]{1,2,0:T(8,128)(2,1)}, u32[]{:S(2)}, u32[]{:S(2)}) async-start(bf16[8,512,288]{1,2,0:T(8,128)(2,1)} %bitcast.55), calls=%async_computation.3 | async-start | bytes 4718592 | tf_op jit(solution)/shard_map/all_to_all | solution.py:20
  1411.4 13.8 copy-start.5
  1440.5 18.4 %slice-start = ((s8[18874368]{0:T(1024)(128)(4,1)}), s8[2097152]{0:T(1024)(128)(4,1)S(1)}, s32[]{:S(2)}) async-start(s8[18874368]{0:T(1024)(128)(4,1)} %bitcast.60), calls=%async_computation.14 | async-start | bytes 4194304
  1440.5 33.8 %all-to-all-start.3 = ((bf16[8,512,288]{1,2,0:T(8,128)(2,1)}), bf16[8,512,288]{1,2,0:T(8,128)(2,1)}, u32[]{:S(2)}, u32[]{:S(2)}) async-start(bf16[8,512,288]{1,2,0:T(8,128)(2,1)} %bitcast.54), calls=%async_computation.6 | async-start | bytes 4718592 | tf_op jit(solution)/shard_map/all_to_all | solution.py:31
  1445.0 13.8 copy-start.3
  1445.0 13.8 slice-start.1
  1445.0 13.8 slice-start.2
  1445.0 13.8 slice-start.3
  1445.1 13.8 slice-start.4
  1466.0 12.6 copy-start.1
Sparse Core Ops, SparseCore 0:
  64.2 223.9 reduce-scatter.7
  291.8 224.6 reduce-scatter.5
  520.1 224.6 reduce-scatter.3
  753.0 98.5 all-gather.3
  853.9 98.5 all-gather.5
  954.8 98.5 all-gather.7
  1074.4 322.6 all-reduce.2
where the time goes:
time: 1490 us
  waiting for transfers between devices  1220 us (82%)
  matrix products  130 us (9%)
  blocking collectives  67.1 us (5%)
  local copies, waits for them, and re-layouts  25.2 us (2%)
  other arithmetic  16.2 us (1%)
    psum x1, waiting for transfers between devices, device_pass(): lax.psum(out_part, 'tp')  323 us
    reduce_scatter x1, waiting for transfers between devices, device_pass(): lax.psum_scatter(gate_part, 'dp', scatter_dimension=0, tiled=True)  228 us
    reduce_scatter x1, waiting for transfers between devices, device_pass(): up_pre = lax.psum_scatter(up_part, 'dp', scatter_dimension=0, tiled=True)  228 us
    reduce_scatter x1, waiting for transfers between devices, device_pass(): grad_h = lax.psum_scatter(grad_part, 'dp', scatter_dimension=0, tiled=True)  150 us
    all_gather x1, waiting for transfers between devices, device_pass(): hidden_all = lax.all_gather(hidden, 'dp', axis=0, tiled=True)  97.5 us
    all_gather x1, waiting for transfers between devices, device_pass(): up_all = lax.all_gather(d_up, 'dp', axis=0, tiled=True)  89.1 us
    all_gather x1, waiting for transfers between devices, device_pass(): gate_all = lax.all_gather(d_gate, 'dp', axis=0, tiled=True)  89.1 us
    all_to_all x1, blocking collectives, device_pass(): dy_cols = lax.all_to_all(dy_rows, 'dp', 1, 0, tiled=True)  34.4 us
  transfers between devices with their start and end apart: 9, of which 9 were waited for; matrix products, arithmetic and copies ran while one was open for 7% of the time, Pallas kernels for 0%

commit v1 on v0

v1 whole, which is shorter than its diff:
```python
import jax
import jax.numpy as jnp
from jax import lax
from jax.sharding import PartitionSpec as P

F32 = jnp.float32
BF16 = jnp.bfloat16


def dot_nn(a, b):
    return jnp.dot(a, b, preferred_element_type=F32)


def dot_nt(a, b):
    return lax.dot_general(a, b, (((1,), (1,)), ((), ())), preferred_element_type=F32)


def dot_tn(a, b):
    return lax.dot_general(a, b, (((0,), (0,)), ((), ())), preferred_element_type=F32)


def hidden_grads(x, dy, wg, wu, wd):
    a = dot_nn(x, wg)
    b = dot_nn(x, wu)
    g = dot_nn(dy, wd)
    s = jax.nn.sigmoid(a)
    silu = a * s
    h = (silu * b).astype(BF16)
    da = (g * b * s * (1.0 + a * (1.0 - s))).astype(BF16)
    db = (g * silu).astype(BF16)
    return h, da, db


def solution(mesh):
    n_tp = mesh.shape['tp']
    n_dp = mesh.shape['dp']

    def device_pass(x_rows, gate_blk, up_blk, down_blk, dy_rows):
        rows = x_rows.shape[0]
        part = rows // n_tp
        tp = lax.axis_index('tp')
        dp = lax.axis_index('dp')
        core = lax.rem(dp, 2)
        wg = lax.all_gather(gate_blk, 'dp', axis=0, tiled=True)
        wu = lax.all_gather(up_blk, 'dp', axis=0, tiled=True)
        wd = lax.all_gather(down_blk.T, 'dp', axis=0, tiled=True)
        x_part = lax.dynamic_slice_in_dim(x_rows, tp * part, part, 0)
        dy_part = lax.dynamic_slice_in_dim(dy_rows, tp * part, part, 0)
        x_all = lax.all_gather(x_part, ('tp', 'dp'), axis=0, tiled=True)
        dy_all = lax.all_gather(dy_part, ('tp', 'dp'), axis=0, tiled=True)

        h, da, db = hidden_grads(x_rows, dy_rows, wg, wu, wd)

        y_part = dot_nt(h, wd)
        dx_part = dot_nt(da, wg) + dot_nt(db, wu)
        y_part, dx_part, x_all, dy_all = lax.optimization_barrier((y_part, dx_part, x_all, dy_all))

        def finish(base, partial):
            mine = lax.psum_scatter(partial, 'tp', scatter_dimension=0, tiled=True)
            out = (base.astype(F32) + mine).astype(BF16)
            return lax.all_gather(out, 'tp', axis=0, tiled=True)

        y = finish(x_part, y_part)
        dx = finish(dy_part, dx_part)

        half = wg.shape[1] // 2
        wg_h = lax.dynamic_slice_in_dim(wg, core * half, half, 1)
        wu_h = lax.dynamic_slice_in_dim(wu, core * half, half, 1)
        wd_h = lax.dynamic_slice_in_dim(wd, core * half, half, 1)
        h, da, db = hidden_grads(x_all, dy_all, wg_h, wu_h, wd_h)
        width = gate_blk.shape[0]
        chip = lax.div(dp, 2)
        x_cols = lax.dynamic_slice_in_dim(x_all, chip * 2 * width, 2 * width, 1)
        dy_cols = lax.dynamic_slice_in_dim(dy_all, chip * 2 * width, 2 * width, 1)
        swap = [(i, i ^ 1) for i in range(n_dp)]

        def exchange(grad, axis):
            own = lax.dynamic_slice_in_dim(grad, core * width, width, axis)
            other = lax.dynamic_slice_in_dim(grad, (1 - core) * width, width, axis)
            other = lax.ppermute(other, 'dp', swap)
            low = jnp.where(core == 0, own, other)
            high = jnp.where(core == 0, other, own)
            return jnp.concatenate([low, high], axis=1 - axis)

        dw_gate = exchange(dot_tn(x_cols, da), 0)
        dw_up = exchange(dot_tn(x_cols, db), 0)
        dw_down = exchange(dot_tn(h, dy_cols), 1)
        return y, dx, dw_gate, dw_up, dw_down

    row_spec = P('dp', None)
    weight_spec = P('dp', 'tp')
    down_spec = P('tp', 'dp')
    return jax.shard_map(device_pass, mesh=mesh,
                         in_specs=(row_spec, weight_spec, weight_spec, down_spec, row_spec),
                         out_specs=(row_spec, row_spec, weight_spec, weight_spec, down_spec),
                         check_vma=False)
```

time: 1490 us -> 755 us (0.51)
  waiting for transfers between devices: 1220 us -> 472 us
  matrix products: 130 us -> 236 us
  blocking collectives: 67.1 us -> 0 us
    reduce_scatter x3 -> x2, waiting for transfers between devices: 606 us -> 8.78 us  [finish(): mine = lax.psum_scatter(partial, 'tp', scatter_dimension=0, tiled=True)]
    psum x1 -> x0, waiting for transfers between devices: 323 us -> none  [device_pass(): lax.psum(out_part, 'tp')]
    all_gather x3 -> x7, waiting for transfers between devices: 276 us -> 460 us  [the longest x1 125 us: device_pass(): dy_all = lax.all_gather(dy_part, ('tp', 'dp'), axis=0, tiled=True)]
    dot_general x9 -> x12, matrix products: 130 us -> 236 us  [the longest x6 127 us: dot_nn(): return jnp.dot(a, b, preferred_element_type=F32)]
    all_to_all x2 -> x0, blocking collectives: 67.1 us -> none  [the longest x1 34.4 us: device_pass(): dy_cols = lax.all_to_all(dy_rows, 'dp', 1, 0, tiled=True)]
    all_to_all x2 -> x0, waiting for transfers between devices: 17.6 us -> none  [the longest x1 13.7 us: device_pass(): y_rows = lax.all_to_all(y_cols, 'dp', 0, 1, tiled=True)]
    unnamed x32 -> x28, local copies, waits for them, and re-layouts: 21.4 us -> 5.88 us
  transfers between devices with their start and end apart: 9 -> 12, of which waited for: 9 -> 8; matrix products, arithmetic and copies ran while one was open for 7% -> 34% of each run, Pallas kernels for 0% -> 0%
where the time goes in v1:
time: 755 us; the launch traced here: 748 us
  waiting for transfers between devices  472 us (63%)
  matrix products  236 us (31%)
  between operations  14.5 us (2%)
  local copies, waits for them, and re-layouts  12.6 us (2%)
  other arithmetic  11.7 us (2%)
    dot_general x6, matrix products, dot_nn(): return jnp.dot(a, b, preferred_element_type=F32)  127 us
    all_gather x1, waiting for transfers between devices, device_pass(): dy_all = lax.all_gather(dy_part, ('tp', 'dp'), axis=0, tiled=True)  125 us
    all_gather x2, waiting for transfers between devices, finish(): return lax.all_gather(out, 'tp', axis=0, tiled=True)  90.6 us
    all_gather x1, waiting for transfers between devices, device_pass(): x_all = lax.all_gather(x_part, ('tp', 'dp'), axis=0, tiled=True)  72.9 us
    dot_general x3, matrix products, dot_tn(): lax.dot_general(a, b, (((0,), (0,)), ((), ())), preferred_element_type=F32)  67.2 us
    all_gather x1, waiting for transfers between devices, device_pass(): wu = lax.all_gather(up_blk, 'dp', axis=0, tiled=True)  62.7 us
    all_gather x1, waiting for transfers between devices, device_pass(): wg = lax.all_gather(gate_blk, 'dp', axis=0, tiled=True)  54.2 us
    all_gather x1, waiting for transfers between devices, device_pass(): wd = lax.all_gather(down_blk.T, 'dp', axis=0, tiled=True)  54.2 us
  transfers between devices with their start and end apart: 12, of which 8 were waited for; matrix products, arithmetic and copies ran while one was open for 34% of the time, Pallas kernels for 0%

profile of v1, /device:TPU:0, one launch (start us, length us, event | category | flops | bytes accessed | tf_op | source)
XLA Modules:
  0.0 747.6 jit_solution(14630089961377584070)
XLA Ops:
  9.4 1.9 constant_dynamic-slice_fusion.4
  11.4 1.9 constant_dynamic-slice_fusion.3
  13.4 62.7 %all-gather.10.cloned.1.call-done = bf16[2304,2304]{1,0:T(8,128)(2,1)} async-done(((bf16[288,2304]{1,0:T(8,128)(2,1)}), bf16[2304,2304]{1,0:T(8,128)(2,1)}) %all-gather.10.cloned.1.call-update) | async-done | bytes 10616848 | tf_op jit(solution)/shard_map/all_gather | solution.py:45
  76.2 11.3 %fusion.33 = f32[512,2304]{1,0:T(8,128)} fusion(bf16[512,2304]{1,0:T(8,128)(2,1)S(1)} %copy-done.4, bf16[2304,2304]{1,0:T(8,128)(2,1)} %all-gather.10.cloned.1.call-done), kind=kOutput, calls=%fused_computation.54 | convolution fusion | flops 5435817984 | bytes 17694720 | tf_op jit(solution)/shard_map/dot_general | solution.py:11
  87.4 54.2 %all-gather.8.cloned.1.call-done = bf16[2304,2304]{1,0:T(8,128)(2,1)} async-done(((bf16[288,2304]{1,0:T(8,128)(2,1)}), bf16[2304,2304]{1,0:T(8,128)(2,1)}) %all-gather.8.cloned.1.call-update) | async-done | bytes 10616848 | tf_op jit(solution)/shard_map/all_gather | solution.py:44
  141.6 11.3 %fusion.32 = f32[512,2304]{1,0:T(8,128)} fusion(bf16[512,2304]{1,0:T(8,128)(2,1)S(1)} %copy-done.4, bf16[2304,2304]{1,0:T(8,128)(2,1)} %all-gather.8.cloned.1.call-done), kind=kOutput, calls=%fused_computation.53 | convolution fusion | flops 5435817984 | bytes 17694720 | tf_op jit(solution)/shard_map/dot_general | solution.py:11
  152.9 54.2 %all-gather.12.cloned.1.call-done = bf16[2304,2304]{1,0:T(8,128)(2,1)} async-done(((bf16[288,2304]{1,0:T(8,128)(2,1)}), bf16[2304,2304]{1,0:T(8,128)(2,1)}) %all-gather.12.cloned.1.call-update) | async-done | bytes 10616848 | tf_op jit(solution)/shard_map/all_gather | solution.py:46
  207.0 11.8 %fusion.34 = f32[512,2304]{1,0:T(8,128)} fusion(bf16[512,2304]{1,0:T(8,128)(2,1)} %param.9, bf16[2304,2304]{1,0:T(8,128)(2,1)} %all-gather.12.cloned.1.call-done), kind=kOutput, calls=%fused_computation.55 | convolution fusion | flops 5435817984 | bytes 17694720 | tf_op jit(solution)/shard_map/dot_general | solution.py:11
  218.9 12.7 %fusion.16 = f32[512,2304]{1,0:T(8,128)} fusion(bf16[2304,2304]{1,0:T(8,128)(2,1)} %all-gather.12.cloned.1.call-done, f32[512,2304]{1,0:T(8,128)} %fusion.33, f32[512,2304]{1,0:T(8,128)S(1)} %copy-done.5), kind=kOutput, calls=%fused_computation.26 | convolution fusion | flops 5442895872 | bytes 24772608 | tf_op jit(solution)/shard_map/dot_general | solution.py:15
  231.6 16.2 %fusion.17 = f32[512,2304]{1,0:T(8,128)} fusion(bf16[2304,2304]{1,0:T(8,128)(2,1)} %all-gather.8.cloned.1.call-done, f32[512,2304]{1,0:T(8,128)} %fusion.32, f32[512,2304]{1,0:T(8,128)} %fusion.34, f32[512,2304]{1,0:T(8,128)} %fusion.33), kind=kOutput, calls=%fused_computation.27 | convolution fusion | flops 5447614464 | bytes 29491200 | tf_op jit(solution)/shard_map/dot_general | solution.py:15
  247.8 13.4 %convolution_add_fusion = f32[512,2304]{1,0:T(8,128)} fusion(f32[512,2304]{1,0:T(8,128)} %fusion.17, bf16[2304,2304]{1,0:T(8,128)(2,1)} %all-gather.10.cloned.1.call-done, f32[512,2304]{1,0:T(8,128)} %fusion.34, f32[512,2304]{1,0:T(8,128)S(1)} %bitcast.17), kind=kOutput, calls=%fused_computation.15 | convolution fusion | flops 5444075520 | bytes 29491200 | tf_op jit(solution)/shard_map/dot_general | solution.py:15
  261.2 72.9 %all-gather.14.cloned.1.call-done = bf16[4096,2304]{1,0:T(8,128)(2,1)} async-done(((bf16[128,2304]{1,0:T(8,128)(2,1)}), bf16[4096,2304]{1,0:T(8,128)(2,1)}) %all-gather.14.cloned.1.call-update) | async-done | bytes 18874384 | tf_op jit(solution)/shard_map/all_gather | solution.py:49
  334.0 125.4 %all-gather.16.cloned.1.call-done = bf16[4096,2304]{1,0:T(8,128)(2,1)} async-done(((bf16[128,2304]{1,0:T(8,128)(2,1)}), bf16[4096,2304]{1,0:T(8,128)(2,1)}) %all-gather.16.cloned.1.call-update) | async-done | bytes 18874384 | tf_op jit(solution)/shard_map/all_gather | solution.py:50
  460.3 31.4 %fusion.4 = f32[4096,1152]{1,0:T(8,128)} fusion(bf16[4096,2304]{1,0:T(8,128)(2,1)} %all-gather.14.cloned.1.call-done, bf16[2304,2304]{1,0:T(8,128)(2,1)} %all-gather.8.cloned.1.call-done, s32[]{:T(128)S(6)} %select_n.58), kind=kOutput, calls=%fused_computation.8 | convolution fusion | flops 21743271936 | bytes 43057156 | tf_op jit(solution)/shard_map/dot_general | solution.py:11
  491.8 31.2 %fusion.6 = f32[4096,1152]{1,0:T(8,128)} fusion(bf16[4096,2304]{1,0:T(8,128)(2,1)} %all-gather.14.cloned.1.call-done, bf16[2304,2304]{1,0:T(8,128)(2,1)} %all-gather.10.cloned.1.call-done, s32[]{:T(128)S(6)} %select_n.58), kind=kOutput, calls=%fused_computation.10 | convolution fusion | flops 21743271936 | bytes 43057156 | tf_op jit(solution)/shard_map/dot_general | solution.py:11
  523.1 29.5 %fusion.8 = f32[4096,1152]{1,0:T(8,128)} fusion(bf16[4096,2304]{1,0:T(8,128)(2,1)S(1)} %bitcast.15, bf16[2304,2304]{1,0:T(8,128)(2,1)} %all-gather.12.cloned.1.call-done, s32[]{:T(128)S(6)} %select_n.58), kind=kOutput, calls=%fused_computation.12 | convolution fusion | flops 21743271936 | bytes 43057156 | tf_op jit(solution)/shard_map/dot_general | solution.py:11
  552.6 25.2 %fusion.3 = f32[576,1152]{1,0:T(8,128)S(1)} fusion(f32[4096,1152]{1,0:T(8,128)} %fusion.4, f32[4096,1152]{1,0:T(8,128)} %fusion.8, f32[4096,1152]{1,0:T(8,128)} %fusion.6, bf16[4096,2304]{1,0:T(8,128)(2,1)} %all-gather.14.cloned.1.call-done, s32[]{:T(128)S(6)} %select_n.57), kind=kOutput, calls=%fused_computation.7 | convolution fusion | flops 5483003904 | bytes 64520196 | tf_op jit(solution)/shard_map/dot_general | solution.py:19
  577.8 1.2 constant_dynamic-slice_fusion.2
  580.0 20.5 %fusion.1 = f32[576,1152]{1,0:T(8,128)S(1)} fusion(f32[4096,1152]{1,0:T(8,128)} %fusion.8, bf16[4096,2304]{1,0:T(8,128)(2,1)} %all-gather.14.cloned.1.call-done, s32[]{:T(128)S(6)} %select_n.57, f32[4096,1152]{1,0:T(8,128)} %fusion.4), kind=kOutput, calls=%fused_computation.5 | convolution fusion | flops 5464129536 | bytes 45645828 | tf_op jit(solution)/shard_map/dot_general | solution.py:19
  600.5 2.3 add_convert_fusion.1
  602.9 21.5 %fusion.2 = f32[1152,576]{0,1:T(8,128)} fusion(f32[4096,1152]{1,0:T(8,128)} %fusion.6, bf16[4096,2304]{1,0:T(8,128)(2,1)} %all-gather.16.cloned.1.call-done, s32[]{:T(128)S(6)} %select_n.57, f32[4096,1152]{1,0:T(8,128)} %fusion.4), kind=kOutput, calls=%fused_computation.6 | convolution fusion | flops 5464129536 | bytes 45645828 | tf_op jit(solution)/shard_map/dot_general | solution.py:19
  624.4 8.8 %reduce-scatter.5.cloned.1.call-done = f32[128,2304]{1,0:T(8,128)} async-done(((f32[512,2304]{1,0:T(8,128)}), f32[128,2304]{1,0:T(8,128)}) %reduce-scatter.5.cloned.1.call-update) | async-done | bytes 1179664 | tf_op jit(solution)/shard_map/reduce_scatter | solution.py:59
  633.2 2.3 add_convert_fusion
  635.8 1.6 constant_dynamic-slice_fusion
  637.7 1.5 dynamic-slice_select_fusion.5
  639.2 1.7 pad_maximum_fusion
  641.3 1.7 pad_maximum_fusion.1
  643.5 1.7 pad_maximum_fusion.2
  645.2 40.5 %all-gather.18.cloned.1.call-done = bf16[512,2304]{1,0:T(8,128)(2,1)} async-done(((bf16[128,2304]{1,0:T(8,128)(2,1)}), bf16[512,2304]{1,0:T(8,128)(2,1)}) %all-gather.18.cloned.1.call-update) | async-done | bytes 2359312 | tf_op jit(solution)/shard_map/all_gather | solution.py:61
  685.7 50.1 %all-gather.20.cloned.1.call-done = bf16[512,2304]{1,0:T(8,128)(2,1)} async-done(((bf16[128,2304]{1,0:T(8,128)(2,1)}), bf16[512,2304]{1,0:T(8,128)(2,1)}) %all-gather.20.cloned.1.call-update) | async-done | bytes 2359312 | tf_op jit(solution)/shard_map/all_gather | solution.py:61
  735.8 3.4 copy.12
  739.2 1.4 copy.13
  (56 shorter events, 5.6 us)
Async XLA Ops:
  7.2 69.0 %copy-start.4 = (bf16[512,2304]{1,0:T(8,128)(2,1)S(1)}, bf16[512,2304]{1,0:T(8,128)(2,1)}, u32[]{:S(2)}) copy-start(bf16[512,2304]{1,0:T(8,128)(2,1)} %param.5) | copy-start | bytes 7077892
  7.2 69.0 %all-gather.10.cloned.1.call-start = ((), (), s32[]{:S(2)}) async-start(), calls=%async_computation.3 | async-start | bytes 11943936 | tf_op jit(solution)/shard_map/all_gather | solution.py:45
  7.9 133.7 %all-gather.8.cloned.1.call-start = ((), (), s32[]{:S(2)}) async-start(), calls=%async_computation.2 | async-start | bytes 11943936 | tf_op jit(solution)/shard_map/all_gather | solution.py:44
  8.7 198.4 %all-gather.12.cloned.1.call-start = ((), (), s32[]{:S(2)}) async-start(), calls=%async_computation.4 | async-start | bytes 11943936 | tf_op jit(solution)/shard_map/all_gather | solution.py:46
  9.4 324.7 %all-gather.14.cloned.1.call-start = ((), (), s32[]{:S(2)}) async-start(), calls=%async_computation.5 | async-start | bytes 19464192 | tf_op jit(solution)/shard_map/all_gather | solution.py:49
  11.4 448.1 %all-gather.16.cloned.1.call-start = ((), (), s32[]{:S(2)}) async-start(), calls=%async_computation.6 | async-start | bytes 19464192 | tf_op jit(solution)/shard_map/all_gather | solution.py:50
  13.4 587.1 %reduce-scatter.3.cloned.1.call-start = ((), (), s32[]{:S(2)}) async-start(), calls=%async_computation.7 | async-start | bytes 5898240 | tf_op jit(solution)/shard_map/reduce_scatter | solution.py:59
  207.0 11.8 %copy-start.5 = (f32[512,2304]{1,0:T(8,128)S(1)}, f32[512,2304]{1,0:T(8,128)}, u32[]{:S(2)}) copy-start(f32[512,2304]{1,0:T(8,128)} %fusion.32) | copy-start | bytes 14155780
  218.9 28.9 %slice-start.5 = ((s8[4718592]{0:T(1024)(128)(4,1)}), s8[524288]{0:T(1024)(128)(4,1)S(1)}, s32[]{:S(2)}) async-start(s8[4718592]{0:T(1024)(128)(4,1)} %bitcast.16), calls=%async_computation.16 | async-start | bytes 1048576
  231.6 16.2 %slice-start.6 = ((s8[4718592]{0:T(1024)(128)(4,1)}), s8[4194304]{0:T(1024)(128)(4,1)S(1)}, s32[]{:S(2)}) async-start(s8[4718592]{0:T(1024)(128)(4,1)} %bitcast.16), calls=%async_computation.17 | async-start | bytes 8388608
  459.5 173.7 %reduce-scatter.5.cloned.1.call-start = ((), (), s32[]{:S(2)}) async-start(), calls=%async_computation.9 | async-start | bytes 5898240 | tf_op jit(solution)/shard_map/reduce_scatter | solution.py:59
  460.3 225.4 %all-gather.18.cloned.1.call-start = ((), (), s32[]{:S(2)}) async-start(), calls=%async_computation.8 | async-start | bytes 2949120 | tf_op jit(solution)/shard_map/all_gather | solution.py:61
  460.3 62.7 %slice-start = ((s8[18874368]{0:T(1024)(128)(4,1)}), s8[4194304]{0:T(1024)(128)(4,1)S(1)}, s32[]{:S(2)}) async-start(s8[18874368]{0:T(1024)(128)(4,1)} %bitcast.14), calls=%async_computation.11 | async-start | bytes 8388608
  460.3 62.7 %slice-start.1 = ((s8[18874368]{0:T(1024)(128)(4,1)}), s8[4194304]{0:T(1024)(128)(4,1)S(1)}, s32[]{:S(2)}) async-start(s8[18874368]{0:T(1024)(128)(4,1)} %bitcast.14), calls=%async_computation.12 | async-start | bytes 8388608
  460.3 62.7 %slice-start.2 = ((s8[18874368]{0:T(1024)(128)(4,1)}), s8[4194304]{0:T(1024)(128)(4,1)S(1)}, s32[]{:S(2)}) async-start(s8[18874368]{0:T(1024)(128)(4,1)} %bitcast.14), calls=%async_computation.13 | async-start | bytes 8388608
  491.8 31.2 %slice-start.3 = ((s8[18874368]{0:T(1024)(128)(4,1)}), s8[4194304]{0:T(1024)(128)(4,1)S(1)}, s32[]{:S(2)}) async-start(s8[18874368]{0:T(1024)(128)(4,1)} %bitcast.14), calls=%async_computation.14 | async-start | bytes 8388608
  491.8 31.3 %slice-start.4 = ((s8[18874368]{0:T(1024)(128)(4,1)}), s8[2097152]{0:T(1024)(128)(4,1)S(1)}, s32[]{:S(2)}) async-start(s8[18874368]{0:T(1024)(128)(4,1)} %bitcast.14), calls=%async_computation.15 | async-start | bytes 4194304
  577.8 1.9 copy-start.1
  579.7 58.0 %collective-permute-start = (f32[288,1152]{1,0:T(8,128)}, f32[288,1152]{1,0:T(8,128)}, u32[]{:S(2)}, u32[]{:S(2)}) collective-permute-start(f32[288,1152]{1,0:T(8,128)} %constant_dynamic-slice_fusion.2), channel_id=1, source_target_pairs={{0,1},{1,0},{2,3},{3,2},{4,5},{5,4},{6,7},{7,6},{8,9},{9,8},{10,11... | collective-permute-start | bytes 3981320 | tf_op jit(solution)/shard_map/ppermute | solution.py:80
  602.9 132.9 %all-gather.20.cloned.1.call-start = ((), (), s32[]{:S(2)}) async-start(), calls=%async_computation.10 | async-start | bytes 2949120 | tf_op jit(solution)/shard_map/all_gather | solution.py:61
  635.6 2.2 copy-start.2
  635.7 5.3 collective-permute-start.1
  637.3 5.6 collective-permute-start.2
  640.9 2.4 copy-start
  735.8 3.4 copy-start.3
Sparse Core Ops, SparseCore 0:
  9.9 66.2 all-gather.9
  78.1 63.4 all-gather.7
  143.5 63.4 all-gather.11
  210.4 123.6 all-gather.13
  337.4 122.0 all-gather.15
  461.6 83.4 reduce-scatter.2
  547.5 85.6 reduce-scatter.4
  635.3 50.2 all-gather.17
  687.2 48.5 all-gather.19

commit v2 on v0

v2 whole, which is shorter than its diff:
```python
import functools

import jax
import jax.numpy as jnp
from jax import lax
from jax.experimental import pallas as pl
from jax.experimental.pallas import tpu as pltpu
from jax.sharding import PartitionSpec as P

F32 = jnp.float32
BF16 = jnp.bfloat16
MESH = pl.DeviceIdType.MESH
SLOTS = 8


def dot_nn(a, b):
    return jnp.dot(a, b, preferred_element_type=F32)


def dot_nt(a, b):
    return lax.dot_general(a, b, (((1,), (1,)), ((), ())), preferred_element_type=F32)


def dot_tn(a, b):
    return lax.dot_general(a, b, (((0,), (0,)), ((), ())), preferred_element_type=F32)


def sigmoid(a):
    return 1.0 / (1.0 + jnp.exp(-a))


def kernel(x_ref, dy_ref, wg_ref, wu_ref, wd_ref,
           yd_ref, og_ref, ou_ref, od_ref, xb, dyb, xp, dyp,
           w_s, acc, yacc, pbuf, sb, xt, dyt, a_s, b_s, g_s, h_all, h_s, da_s, db_s, rbuf, fin,
           w_send, w_recv, wr_send, wr_recv, w_own, wp_send, wp_recv,
           own_send, own_recv, q_send, q_recv, rl_send, f_send, f_recv,
           sb_send, sb_recv, credit, rs_send, rs_recv, ag_send, ag_recv, fin_own, ld, out_send, out_recv, out_own):
    rows, model = x_ref.shape
    blk, width = wg_ref.shape
    half = width // 2
    hb = blk // 2
    tile = rows // 2
    piece = tile // 4
    rc = rows // 32
    steps = 16
    win = acc.shape[1]
    w_in = (wg_ref, wu_ref, wd_ref)
    outs = (og_ref, ou_ref, od_ref)
    tok = (x_ref, dy_ref)
    tok_b = (xb, dyb)
    tok_p = (xp, dyp)
    tok_t = (xt, dyt)

    t = lax.axis_index('tp')
    me = lax.axis_index('dp')
    cy = lax.div(me, 4)
    cx = lax.rem(lax.div(me, 2), 2)
    j = lax.rem(me, 2)
    partner = me + 1 - 2 * j
    chip = cy * 2 + cx

    def near(link, core):
        if link == 0:
            return cy * 4 + (1 - cx) * 2 + core
        return (1 - cy) * 4 + cx * 2 + core

    def far(core):
        return (1 - cy) * 4 + (1 - cx) * 2 + core

    def send(src, dst, s_sem, r_sem, dp=None, tp=None):
        where = {'dp': me if dp is None else dp, 'tp': t if tp is None else tp}
        return pltpu.make_async_remote_copy(src_ref=src, dst_ref=dst, send_sem=s_sem, recv_sem=r_sem,
                                            device_id=where, device_id_type=MESH)

    def wait(ref, sem):
        pltpu.make_async_copy(ref, ref, sem).wait()

    barrier = pltpu.get_barrier_semaphore()
    for peer in (partner, near(0, 0), near(0, 1), near(1, 0), near(1, 1)):
        pl.semaphore_signal(barrier, inc=1, device_id={'dp': peer, 'tp': t}, device_id_type=MESH)

    @pl.when(t > 0)
    def _():
        pl.semaphore_signal(barrier, inc=1, device_id={'dp': me, 'tp': t - 1}, device_id_type=MESH)

    @pl.when(t < 3)
    def _():
        pl.semaphore_signal(barrier, inc=1, device_id={'dp': me, 'tp': t + 1}, device_id_type=MESH)

    pl.semaphore_wait(barrier, 5 + jnp.minimum(t, 1) + jnp.minimum(3 - t, 1))

    def w_rows(k, dev, part=None):
        if part is None:
            return w_s.at[k, pl.ds(pl.multiple_of(dev * blk, 16), blk), :]
        return w_s.at[k, pl.ds(pl.multiple_of(dev * blk + part * hb, 16), hb), :]

    def w_cols(core):
        return pl.ds(pl.multiple_of(core * half, 128), half)

    def w_copy(k, link, part, core):
        return send(w_in[k].at[pl.ds(part * hb, hb), w_cols(core)], w_rows(k, me, part),
                    w_send.at[k, link, part, core], w_recv.at[k, link, part, j], dp=near(link, core))

    def w_own_copy(k):
        return pltpu.make_async_copy(w_in[k].at[:, w_cols(j)], w_rows(k, me), w_own.at[k])

    def w_partner_copy(k):
        return send(w_in[k].at[:, w_cols(1 - j)], w_rows(k, me), wp_send.at[k], wp_recv.at[k], dp=partner)

    def w_start(k):
        for first in (0, 1):
            for core in (0, 1):
                w_copy(k, 0, 1 - first, core).start()
                w_copy(k, 1, first, core).start()
        w_own_copy(k).start()
        w_partner_copy(k).start()

    def w_relay_copy(k, link_out, core):
        part = 1 if link_out == 1 else 0
        ref = w_rows(k, near(1 - link_out, core), part)
        return send(ref, ref, wr_send.at[k, link_out, core], wr_recv.at[k, link_out, core], dp=near(link_out, j))

    def w_relay(k):
        for core in (0, 1):
            wait(w_rows(k, near(0, core), 1), w_recv.at[k, 0, 1, core])
            w_relay_copy(k, 1, core).start()
            wait(w_rows(k, near(1, core), 0), w_recv.at[k, 1, 0, core])
            w_relay_copy(k, 0, core).start()

    def w_finish(k):
        for core in (0, 1):
            wait(w_rows(k, near(0, core), 0), w_recv.at[k, 0, 0, core])
            wait(w_rows(k, near(1, core), 1), w_recv.at[k, 1, 1, core])
        wait(w_rows(k, me), w_own.at[k])
        wait(w_rows(k, partner), wp_recv.at[k])
        for core in (0, 1):
            wait(w_rows(k, far(core), 0), wr_recv.at[k, 0, core])
            wait(w_rows(k, far(core), 1), wr_recv.at[k, 1, core])

    def slot_of(ten, q, link, core):
        return tok_b[ten].at[q, pl.ds(pl.multiple_of((2 * link + core) * piece, piece), piece), :]

    def q_copy(ten, q, link):
        b = lax.div(q, 4)
        sub = lax.rem(q, 4)
        first = 1 - b if link == 0 else b
        src = tok[ten].at[pl.ds(pl.multiple_of(first * tile + sub * piece, piece), piece), :]
        return send(src, slot_of(ten, q, link, j), q_send.at[q, link, ten], q_recv.at[q, link, ten], dp=near(link, j))

    def relay_copy(ten, sub, link_out):
        return send(slot_of(ten, sub, 1 - link_out, j), slot_of(ten, 8 + sub, link_out, j),
                    rl_send.at[sub, link_out, ten], q_recv.at[8 + sub, link_out, ten], dp=near(link_out, j))

    def forward_copy(ten, q, link):
        ref = slot_of(ten, q, link, j)
        return send(ref, ref, f_send.at[q, link, ten], f_recv.at[q, link, ten], dp=partner)

    def own_copy(ten):
        return send(tok[ten], tok_p[ten], own_send.at[ten], own_recv.at[ten], dp=partner)

    def chunk(ten, s, way):
        row = (lax.rem(s, steps) * 2 + way) * rc
        return ten, pl.ds(pl.multiple_of(row, rc), rc), slice(None)

    def sum_copy(s, way, nxt):
        slot = lax.rem(s, SLOTS)
        return send(yacc.at[chunk(lax.div(s, steps), s, way)], rbuf.at[way, slot],
                    rs_send.at[way, slot], rs_recv.at[way, slot], tp=nxt)

    def done_copy(s, way, prv, src):
        slot = lax.rem(s, SLOTS)
        return send(src, yd_ref.at[chunk(lax.div(s, steps), s, way)], ag_send.at[way, slot], ag_recv.at[way, slot], tp=prv)

    def tick(tau):
        for way in (0, 1):
            p = t if way == 0 else 3 - t
            nxt = t + 1 if way == 0 else t - 1
            prv = t - 1 if way == 0 else t + 1
            s = tau - p
            slot = lax.rem(jnp.maximum(s, 0), SLOTS)
            live = jnp.logical_and(s >= 0, s < 2 * steps)

            @pl.when(jnp.logical_and(live, p > 0))
            def _():
                wait(rbuf.at[way, slot], rs_recv.at[way, slot])

            @pl.when(jnp.logical_and(live, p < 3))
            def _():
                @pl.when(s >= SLOTS)
                def _():
                    sum_copy(s - SLOTS, way, nxt).wait_send()

                @pl.when(p > 0)
                def _():
                    here = chunk(lax.div(s, steps), s, way)
                    yacc[here] = yacc[here] + rbuf[way, slot]

                sum_copy(s, way, nxt).start()

            @pl.when(jnp.logical_and(live, p == 3))
            def _():
                @pl.when(s >= SLOTS)
                def _():
                    done_copy(s - SLOTS, way, prv, fin.at[way, slot]).wait_send()
                    wait(fin.at[way, slot], fin_own.at[way, slot])

                here = chunk(lax.div(s, steps), s, way)
                fin[way, slot] = (yacc[here] + rbuf[way, slot]).astype(BF16)
                pltpu.make_async_copy(fin.at[way, slot], yd_ref.at[here], fin_own.at[way, slot]).start()
                done_copy(s, way, prv, fin.at[way, slot]).start()

            s2 = tau - 6 + p
            slot2 = lax.rem(jnp.maximum(s2, 0), SLOTS)
            live2 = jnp.logical_and(jnp.logical_and(s2 >= 0, s2 < 2 * steps), p < 3)

            @pl.when(live2)
            def _():
                here = yd_ref.at[chunk(lax.div(s2, steps), s2, way)]
                wait(here, ag_recv.at[way, slot2])

                @pl.when(p > 0)
                def _():
                    @pl.when(s2 >= SLOTS)
                    def _():
                        done_copy(s2 - SLOTS, way, prv, here).wait_send()

                    done_copy(s2, way, prv, here).start()

    def drain_sums():
        def body(n, carry):
            s = 2 * steps - SLOTS + n
            for way in (0, 1):
                p = t if way == 0 else 3 - t
                slot = lax.rem(s, SLOTS)

                @pl.when(p < 3)
                def _():
                    wait(rbuf.at[way, slot], rs_send.at[way, slot])

                @pl.when(p > 0)
                def _():
                    wait(fin.at[way, slot], ag_send.at[way, slot])

                @pl.when(p == 3)
                def _():
                    wait(fin.at[way, slot], fin_own.at[way, slot])
            return carry

        lax.fori_loop(0, SLOTS, body, 0)

    w_start(0)
    w_start(1)
    for ten in (0, 1):
        own_copy(ten).start()

    def clear(n, carry):
        at = pl.ds(pl.multiple_of(n * 32, 32), 32)
        for k in range(3):
            acc[k, at, :] = jnp.zeros((32, half), F32)
        return carry

    lax.fori_loop(0, win // 32, clear, 0)
    w_relay(0)
    w_relay(1)
    w_start(2)
    w_finish(0)
    w_finish(1)

    group = min(32, tile)
    first = pl.multiple_of(lax.div(chip * 2 * blk, 128) * 128, 128)
    shift = chip * 2 * blk - first
    cols = pl.ds(first, win)
    base = jnp.where(t == 0, 1.0, 0.0).astype(F32)

    def put_partial(ten, r, own):
        at = pl.ds(pl.multiple_of(r * tile, tile), tile)

        @pl.when(own == 0)
        def _():
            if ten == 1:
                pl.semaphore_wait(credit, 1)
            send(sb.at[0], pbuf.at[at, :], sb_send.at[ten, r], sb_recv.at[ten, r], dp=partner).start()

        @pl.when(own == 1)
        def _():
            wait(pbuf.at[at, :], sb_recv.at[ten, r])
            src = tok_t[ten]

            def body(n, carry):
                lo = pl.ds(pl.multiple_of(n * group, group), group)
                there = pl.ds(pl.multiple_of(r * tile + n * group, group), group)
                yacc[ten, there, :] = sb[1, lo, :] + pbuf[there, :] + src[lo, :].astype(F32) * base
                return carry

            lax.fori_loop(0, tile // group, body, 0)
            if ten == 0:
                pl.semaphore_signal(credit, inc=1, device_id={'dp': partner, 'tp': t}, device_id_type=MESH)

    def free_sb(ten, r, own):
        if ten == 1:
            @pl.when(jnp.logical_and(own == 0, r == 0))
            def _():
                wait(sb.at[0], sb_send.at[0, 1])

        @pl.when(jnp.logical_and(own == 0, r == 1))
        def _():
            wait(sb.at[0], sb_send.at[ten, 0])

    n_block = 3
    n_cols = model // n_block

    def one_tile(i, carry):
        r = lax.div(lax.rem(i, 4), 2)
        own = lax.rem(i, 2)
        q = i - 12

        @pl.when(i == 2)
        def _():
            w_relay(2)

        @pl.when(jnp.logical_and(i >= 2, i < 10))
        def _():
            for ten in (0, 1):
                for link in (0, 1):
                    q_copy(ten, i - 2, link).start()

        @pl.when(i == 4)
        def _():
            w_finish(2)

        at = pl.ds(pl.multiple_of(r * tile, tile), tile)
        for ten in (0, 1):
            due = i < 12 if ten == 0 else jnp.logical_and(i >= 8, i < 12)

            @pl.when(jnp.logical_and(due, own == 1))
            def _():
                pltpu.make_async_copy(tok[ten].at[at, :], tok_t[ten], ld.at[ten]).start()

            @pl.when(i == 8 * ten)
            def _():
                wait(tok_p[ten], own_recv.at[ten])

            @pl.when(jnp.logical_and(due, own == 0))
            def _():
                pltpu.make_async_copy(tok_p[ten].at[at, :], tok_t[ten], ld.at[ten]).start()

        @pl.when(i >= 12)
        def _():
            for ten in (0, 1):
                for link in (0, 1):
                    wait(slot_of(ten, q, link, j), q_recv.at[q, link, ten])
                    forward_copy(ten, q, link).start()

            @pl.when(q < 4)
            def _():
                for ten in (0, 1):
                    for link in (0, 1):
                        relay_copy(ten, q, link).start()

            for ten in (0, 1):
                for link in (0, 1):
                    wait(slot_of(ten, q, link, 1 - j), f_recv.at[q, link, ten])
                pltpu.make_async_copy(tok_b[ten].at[q], tok_t[ten], ld.at[ten]).start()

        wait(xt, ld.at[0])

        @pl.when(jnp.logical_or(i < 4, i >= 8))
        def _():
            a_s[...] = dot_nn(xt[...], w_s[0])
            b_s[...] = dot_nn(xt[...], w_s[1])
            tick(jnp.where(i >= 12, 15 + 2 * (i - 12), jnp.where(i >= 8, 3 + 3 * (i - 8), -1000)))

        @pl.when(i < 4)
        def _():
            def body(n, c):
                lo = pl.ds(pl.multiple_of(n * group, group), group)
                a = a_s[lo, :]
                h_all[i, lo, :] = (a * sigmoid(a) * b_s[lo, :]).astype(BF16)
                return c

            lax.fori_loop(0, tile // group, body, 0)

        @pl.when(jnp.logical_and(i >= 4, i < 8))
        def _():
            free_sb(0, r, own)

            def block(n, c):
                to = pl.ds(pl.multiple_of(n * n_cols, n_cols), n_cols)
                sb[own, :, to] = dot_nt(h_all[lax.rem(i, 4)], w_s[2, to, :])
                return c

            lax.fori_loop(0, n_block, block, 0)
            put_partial(0, r, own)
            tick(jnp.where(i >= 5, i - 5, -1000))

        @pl.when(i >= 8)
        def _():
            wait(dyt, ld.at[1])
            g_s[...] = dot_nn(dyt[...], w_s[2])

            def body(n, c):
                lo = pl.ds(pl.multiple_of(n * group, group), group)
                a = a_s[lo, :]
                b = b_s[lo, :]
                g = g_s[lo, :]
                s = sigmoid(a)
                silu = a * s
                h_s[lo, :] = (silu * b).astype(BF16)
                da_s[lo, :] = (g * b * s * (1.0 + a * (1.0 - s))).astype(BF16)
                db_s[lo, :] = (g * silu).astype(BF16)
                return c

            lax.fori_loop(0, tile // group, body, 0)
            x_win = xt[:, cols]
            acc[0] += dot_tn(x_win, da_s[...])
            acc[1] += dot_tn(x_win, db_s[...])
            acc[2] += dot_tn(dyt[:, cols], h_s[...])

            tick(jnp.where(i >= 12, 16 + 2 * (i - 12), 4 + 3 * (i - 8)))

        @pl.when(jnp.logical_and(i >= 8, i < 12))
        def _():
            free_sb(1, r, own)

            def block(n, c):
                to = pl.ds(pl.multiple_of(n * n_cols, n_cols), n_cols)
                sb[own, :, to] = dot_nt(da_s[...], w_s[0, to, :]) + dot_nt(db_s[...], w_s[1, to, :])
                return c

            lax.fori_loop(0, n_block, block, 0)
            put_partial(1, r, own)
            tick(5 + 3 * (i - 8))

        return carry

    lax.fori_loop(0, 24, one_tile, 0)

    def w_grad(k, core):
        return acc.at[k, pl.ds(pl.multiple_of(shift + core * blk, 8), blk), :]

    for k in range(3):
        send(w_grad(k, 1 - j), outs[k].at[:, w_cols(j)], out_send.at[k], out_recv.at[k], dp=partner).start()
        pltpu.make_async_copy(w_grad(k, j), outs[k].at[:, w_cols(j)], out_own.at[k]).start()

    drain_sums()
    wait(sb.at[0], sb_send.at[1, 1])
    for k in range(3):
        for core in (0, 1):
            for link in (0, 1):
                for part in (0, 1):
                    w_copy(k, link, part, core).wait_send()
                w_relay_copy(k, link, core).wait_send()
        w_partner_copy(k).wait_send()
    for ten in (0, 1):
        own_copy(ten).wait_send()

    def drain(q, carry):
        for ten in (0, 1):
            for link in (0, 1):
                @pl.when(q < 8)
                def _():
                    wait(slot_of(ten, 0, link, j), q_send.at[lax.rem(q, 8), link, ten])

                @pl.when(q < 4)
                def _():
                    wait(slot_of(ten, 0, link, j), rl_send.at[lax.rem(q, 4), link, ten])

                wait(slot_of(ten, q, link, j), f_send.at[q, link, ten])
        return carry

    lax.fori_loop(0, 12, drain, 0)
    for k in range(3):
        wait(w_grad(k, j), out_own.at[k])
        wait(w_grad(k, 1 - j), out_send.at[k])
        wait(w_grad(k, j), out_recv.at[k])


def window(model, blk):
    starts = [(2 * blk * c) // 128 * 128 for c in range(model // (2 * blk))]
    shift = max(2 * blk * c - s for c, s in enumerate(starts))
    return -(-(shift + 2 * blk) // 128) * 128


def mega(x, dy, wg, wu, wd):
    rows, model = x.shape
    blk, width = wg.shape
    half = width // 2
    tile = rows // 2
    rc = rows // 32
    dma = pltpu.SemaphoreType.DMA
    anywhere = pl.BlockSpec(memory_space=pl.ANY)
    shape = jax.ShapeDtypeStruct
    flops = 2 * model * half * rows * 2 * 20
    return pl.pallas_call(
        kernel,
        name='mlp',
        out_shape=(shape((2, rows, model), BF16),
                   shape((blk, width), F32), shape((blk, width), F32), shape((blk, width), F32),
                   shape((12, tile, model), BF16), shape((12, tile, model), BF16),
                   shape((rows, model), BF16), shape((rows, model), BF16)),
        in_specs=[anywhere] * 5,
        out_specs=tuple([anywhere] * 8),
        scratch_shapes=[
            pltpu.VMEM((3, model, half), BF16),
            pltpu.VMEM((3, window(model, blk), half), F32),
            pltpu.VMEM((2, rows, model), F32),
            pltpu.VMEM((rows, model), F32),
            pltpu.VMEM((2, tile, model), F32),
            pltpu.VMEM((tile, model), BF16),
            pltpu.VMEM((tile, model), BF16),
            pltpu.VMEM((tile, half), F32),
            pltpu.VMEM((tile, half), F32),
            pltpu.VMEM((tile, half), F32),
            pltpu.VMEM((4, tile, half), BF16),
            pltpu.VMEM((tile, half), BF16),
            pltpu.VMEM((tile, half), BF16),
            pltpu.VMEM((tile, half), BF16),
            pltpu.VMEM((2, SLOTS, rc, model), F32),
            pltpu.VMEM((2, SLOTS, rc, model), BF16),
            dma((3, 2, 2, 2)), dma((3, 2, 2, 2)), dma((3, 2, 2)), dma((3, 2, 2)), dma((3,)), dma((3,)), dma((3,)),
            dma((2,)), dma((2,)), dma((8, 2, 2)), dma((12, 2, 2)), dma((4, 2, 2)), dma((12, 2, 2)), dma((12, 2, 2)),
            dma((2, 2)), dma((2, 2)), pltpu.SemaphoreType.REGULAR,
            dma((2, SLOTS)), dma((2, SLOTS)), dma((2, SLOTS)), dma((2, SLOTS)), dma((2, SLOTS)),
            dma((2,)), dma((3,)), dma((3,)), dma((3,)),
        ],
        compiler_params=pltpu.CompilerParams(collective_id=0, has_side_effects=True, vmem_limit_bytes=67_000_000),
        cost_estimate=pl.CostEstimate(flops=flops, bytes_accessed=100_000_000, transcendentals=0),
    )(x, dy, wg, wu, wd)


def solution(mesh):
    def device_pass(x_rows, gate_blk, up_blk, down_blk, dy_rows):
        out = mega(x_rows, dy_rows, gate_blk, up_blk, down_blk.T)
        yd, dw_gate, dw_up, dw_down = out[:4]
        return yd[0], yd[1], dw_gate, dw_up, dw_down.T

    row_spec = P('dp', None)
    weight_spec = P('dp', 'tp')
    down_spec = P('tp', 'dp')
    return jax.shard_map(device_pass, mesh=mesh,
                         in_specs=(row_spec, weight_spec, weight_spec, down_spec, row_spec),
                         out_specs=(row_spec, row_spec, weight_spec, weight_spec, down_spec),
                         check_vma=False)
```

time: 1490 us -> 384 us (0.26)
  waiting for transfers between devices: 1220 us -> 0 us
  Pallas kernels: 0 us -> 371 us
  matrix products: 130 us -> 0 us
  blocking collectives: 67.1 us -> 0 us
  other arithmetic: 16.2 us -> 0 us
    reduce_scatter x3 -> x0, waiting for transfers between devices: 606 us -> none  [the longest x1 228 us: device_pass(): lax.psum_scatter(gate_part, 'dp', scatter_dimension=0, tiled=True)]
    pallas_call x0 -> x1, Pallas kernels: none -> 371 us  [mega(): pl.pallas_call(kernel, name='mlp', out_shape=(shape((2, rows, model), BF1...]
    psum x1 -> x0, waiting for transfers between devices: 323 us -> none  [device_pass(): lax.psum(out_part, 'tp')]
    all_gather x3 -> x0, waiting for transfers between devices: 276 us -> none  [the longest x1 97.5 us: device_pass(): hidden_all = lax.all_gather(hidden, 'dp', axis=0, tiled=True)]
    dot_general x9 -> x0, matrix products: 130 us -> none  [the longest x1 21 us: device_pass(): jnp.einsum('tf,df->td', up_all, up_blk, preferred_element_type=jnp.float32)]
    all_to_all x2 -> x0, blocking collectives: 67.1 us -> none  [the longest x1 34.4 us: device_pass(): dy_cols = lax.all_to_all(dy_rows, 'dp', 1, 0, tiled=True)]
    all_to_all x2 -> x0, waiting for transfers between devices: 17.6 us -> none  [the longest x1 13.7 us: device_pass(): y_rows = lax.all_to_all(y_cols, 'dp', 0, 1, tiled=True)]
    convert_element_type x2 -> x0, other arithmetic: 16.2 us -> none  [the longest x1 8.1 us: device_pass(): d_up = (grad_h * silu_gate).astype(jnp.bfloat16)]
  transfers between devices with their start and end apart: 9 -> 0, of which waited for: 9 -> 0; matrix products, arithmetic and copies ran while one was open for 7% -> 0% of each run, Pallas kernels for 0% -> 0%
where the time goes in v2:
time: 384 us; the launch traced here: 383 us
  Pallas kernels  371 us (97%)
  local copies, waits for them, and re-layouts  11.9 us (3%)
    pallas_call x1, Pallas kernels, mega(): pl.pallas_call(kernel, name='mlp', out_shape=(shape((2, rows, model), BF1...  371 us

profile of v2, /device:TPU:0, one launch (start us, length us, event | category | flops | bytes accessed | tf_op | source)
XLA Modules:
  0.0 383.2 jit_solution(9890597753043031162)
XLA Ops:
  0.6 370.6 %mlp.1 = (bf16[2,512,2304]{2,1,0:T(8,128)(2,1)}, f32[288,2304]{1,0:T(8,128)}, f32[288,2304]{1,0:T(8,128)}, f32[288,2304]{1,0:T(8,128)}, bf16[12,256,2304]{2,1,0:...) custom-call(bf16[512,2304]{1,0:T(8,128)(2,1)} %x_ref.1, ...), custom_call_target="tpu_custom_call" | custom-call | flops 108716359680 | bytes 100000000 | tf_op jit(solution)/shard_map/mlp/pallas_call | solution.py:494
  371.2 0.0 copy-start.2
  371.2 5.0 %slice_bitcast_fusion = (bf16[512,2304]{1,0:T(8,128)(2,1)}, bf16[512,2304]{1,0:T(8,128)(2,1)}) fusion(bf16[2,512,2304]{2,1,0:T(8,128)(2,1)} %get-tuple-element.9), kind=kLoop, calls=%fused_computation | loop fusion | bytes 9437184 | tf_op jit(solution)/shard_map/squeeze | solution.py:535
  376.3 0.0 copy-done.2
  376.3 0.0 copy-start.1
  376.3 1.5 copy.13
  377.8 1.2 copy-done.1
  379.0 0.0 copy-start
  379.0 1.5 copy.14
  380.5 1.2 copy-done
  381.7 1.5 copy.15
Async XLA Ops:
  371.2 5.0 %copy-start.2 = (f32[288,2304]{1,0:T(8,128)S(1)}, f32[288,2304]{1,0:T(8,128)}, u32[]{:S(2)}) copy-start(f32[288,2304]{1,0:T(8,128)} %get-tuple-element.22) | copy-start | bytes 7962628
  376.3 2.7 copy-start.1
  379.0 2.7 copy-start

commit v3 on v2

v3 whole, which is shorter than its diff:
```python
import jax
import jax.numpy as jnp
from jax import lax
from jax.experimental import pallas as pl
from jax.experimental.pallas import tpu as pltpu
from jax.sharding import PartitionSpec as P

F32 = jnp.float32
BF16 = jnp.bfloat16
MESH = pl.DeviceIdType.MESH
SLOTS = 8
LANES = 128


def dot_nn(a, b):
    return jnp.dot(a, b, preferred_element_type=F32)


def dot_nt(a, b):
    return lax.dot_general(a, b, (((1,), (1,)), ((), ())), preferred_element_type=F32)


def dot_tn(a, b):
    return lax.dot_general(a, b, (((0,), (0,)), ((), ())), preferred_element_type=F32)


def sigmoid(a):
    return 1.0 / (1.0 + jnp.exp(-a))


def kernel(x_ref, dy_ref, wg_ref, wu_ref, wd_ref,
           yd_ref, og_ref, ou_ref, od_ref, xb, dyb, xp, dyp,
           w_s, acc, yacc, pbuf, sb, xt, dyt, a_all, b_all, g_s, h_all, rbuf, fin,
           w_send, w_recv, wr_send, wr_recv, w_own, wp_send, wp_recv,
           own_send, own_recv, q_send, q_recv, rl_send, f_send, f_recv,
           y_send, y_recv, dx_send, dx_recv, credit,
           rs_send, rs_recv, ag_send, ag_recv, fin_own, ld, out_send, out_recv, out_own):
    rows, model = x_ref.shape
    blk, width = wg_ref.shape
    half = width // 2
    hb = blk // 2
    tile = rows // 2
    piece = tile // 4
    win = acc.shape[1]
    line = model // 2
    units = line // LANES
    near_units = (2 * blk - LANES // 2) // LANES if (2 * blk) % LANES else 2 * blk // LANES
    rest_units = units - near_units
    steps = 2 * units
    group = min(32, tile)
    w_in = (wg_ref, wu_ref, wd_ref)
    outs = (og_ref, ou_ref, od_ref)
    tok = (x_ref, dy_ref)
    tok_b = (xb, dyb)
    tok_p = (xp, dyp)
    tok_t = (xt, dyt)

    t = lax.axis_index('tp')
    me = lax.axis_index('dp')
    cy = lax.div(me, 4)
    cx = lax.rem(lax.div(me, 2), 2)
    j = lax.rem(me, 2)
    partner = me + 1 - 2 * j
    chip = cy * 2 + cx

    def near(link, core):
        if link == 0:
            return cy * 4 + (1 - cx) * 2 + core
        return (1 - cy) * 4 + cx * 2 + core

    def far(core):
        return (1 - cy) * 4 + (1 - cx) * 2 + core

    def send(src, dst, s_sem, r_sem, dp=None, tp=None):
        where = {'dp': me if dp is None else dp, 'tp': t if tp is None else tp}
        return pltpu.make_async_remote_copy(src_ref=src, dst_ref=dst, send_sem=s_sem, recv_sem=r_sem,
                                            device_id=where, device_id_type=MESH)

    def wait(ref, sem):
        pltpu.make_async_copy(ref, ref, sem).wait()

    barrier = pltpu.get_barrier_semaphore()
    for peer in (partner, near(0, 0), near(0, 1), near(1, 0), near(1, 1)):
        pl.semaphore_signal(barrier, inc=1, device_id={'dp': peer, 'tp': t}, device_id_type=MESH)

    @pl.when(t > 0)
    def _():
        pl.semaphore_signal(barrier, inc=1, device_id={'dp': me, 'tp': t - 1}, device_id_type=MESH)

    @pl.when(t < 3)
    def _():
        pl.semaphore_signal(barrier, inc=1, device_id={'dp': me, 'tp': t + 1}, device_id_type=MESH)

    pl.semaphore_wait(barrier, 5 + jnp.minimum(t, 1) + jnp.minimum(3 - t, 1))

    def w_rows(k, dev, part=None):
        if part is None:
            return w_s.at[k, pl.ds(pl.multiple_of(dev * blk, 16), blk), :]
        return w_s.at[k, pl.ds(pl.multiple_of(dev * blk + part * hb, 16), hb), :]

    def w_cols(core):
        return pl.ds(pl.multiple_of(core * half, LANES), half)

    def w_copy(k, link, part, core):
        return send(w_in[k].at[pl.ds(part * hb, hb), w_cols(core)], w_rows(k, me, part),
                    w_send.at[k, link, part, core], w_recv.at[k, link, part, j], dp=near(link, core))

    def w_own_copy(k):
        return pltpu.make_async_copy(w_in[k].at[:, w_cols(j)], w_rows(k, me), w_own.at[k])

    def w_partner_copy(k):
        return send(w_in[k].at[:, w_cols(1 - j)], w_rows(k, me), wp_send.at[k], wp_recv.at[k], dp=partner)

    def w_start(k):
        for first in (0, 1):
            for core in (0, 1):
                w_copy(k, 0, 1 - first, core).start()
                w_copy(k, 1, first, core).start()
        w_own_copy(k).start()
        w_partner_copy(k).start()

    def w_relay_copy(k, link_out, core):
        part = 1 if link_out == 1 else 0
        ref = w_rows(k, near(1 - link_out, core), part)
        return send(ref, ref, wr_send.at[k, link_out, core], wr_recv.at[k, link_out, core], dp=near(link_out, j))

    def w_relay(k):
        for core in (0, 1):
            wait(w_rows(k, near(0, core), 1), w_recv.at[k, 0, 1, core])
            w_relay_copy(k, 1, core).start()
            wait(w_rows(k, near(1, core), 0), w_recv.at[k, 1, 0, core])
            w_relay_copy(k, 0, core).start()

    def w_have(k, which):
        if which == 'chip':
            wait(w_rows(k, me), w_own.at[k])
            wait(w_rows(k, partner), wp_recv.at[k])
        for core in (0, 1):
            if which == 'x':
                wait(w_rows(k, near(0, core), 0), w_recv.at[k, 0, 0, core])
            if which == 'y':
                wait(w_rows(k, near(1, core), 1), w_recv.at[k, 1, 1, core])
            if which == 'far':
                wait(w_rows(k, far(core), 0), wr_recv.at[k, 0, core])
                wait(w_rows(k, far(core), 1), wr_recv.at[k, 1, core])

    def slot_of(ten, q, link, core):
        return tok_b[ten].at[q, pl.ds(pl.multiple_of((2 * link + core) * piece, piece), piece), :]

    def q_copy(ten, q, link):
        b = lax.div(q, 4)
        sub = lax.rem(q, 4)
        first = 1 - b if link == 0 else b
        src = tok[ten].at[pl.ds(pl.multiple_of(first * tile + sub * piece, piece), piece), :]
        return send(src, slot_of(ten, q, link, j), q_send.at[q, link, ten], q_recv.at[q, link, ten], dp=near(link, j))

    def q_start(q):
        for ten in (0, 1):
            for link in (0, 1):
                q_copy(ten, q, link).start()

    def relay_copy(ten, sub, link_out):
        return send(slot_of(ten, sub, 1 - link_out, j), slot_of(ten, 8 + sub, link_out, j),
                    rl_send.at[sub, link_out, ten], q_recv.at[8 + sub, link_out, ten], dp=near(link_out, j))

    def forward_copy(ten, q, link):
        ref = slot_of(ten, q, link, j)
        return send(ref, ref, f_send.at[q, link, ten], f_recv.at[q, link, ten], dp=partner)

    def own_copy(ten):
        return send(tok[ten], tok_p[ten], own_send.at[ten], own_recv.at[ten], dp=partner)

    def arrive(ten, q):
        with jax.named_scope('arrive'):
            for link in (0, 1):
                wait(slot_of(ten, q, link, j), q_recv.at[q, link, ten])
                forward_copy(ten, q, link).start()

        @pl.when(q < 4)
        def _():
            for link in (0, 1):
                relay_copy(ten, q, link).start()

    def load_b(ten, q):
        with jax.named_scope('passed'):
            for link in (0, 1):
                wait(slot_of(ten, q, link, 1 - j), f_recv.at[q, link, ten])
        pltpu.make_async_copy(tok_b[ten].at[q], tok_t[ten].at[lax.rem(q, 2)], ld.at[ten, lax.rem(q, 2)]).start()

    def rows_of(r):
        return pl.ds(pl.multiple_of(r * tile, tile), tile)

    def load_a(ten, n):
        own = lax.div(n, 2)
        slot = lax.rem(n, 2)

        @pl.when(own == 1)
        def _():
            pltpu.make_async_copy(tok[ten].at[rows_of(slot), :], tok_t[ten].at[slot], ld.at[ten, slot]).start()

        @pl.when(own == 0)
        def _():
            pltpu.make_async_copy(tok_p[ten].at[rows_of(slot), :], tok_t[ten].at[slot], ld.at[ten, slot]).start()

    def loaded(ten, slot):
        with jax.named_scope('ld'):
            wait(tok_t[ten].at[slot], ld.at[ten, slot])

    def unit_col(u):
        mine = cy * units
        other = (1 - cy) * units
        low = cx * rest_units
        high = (1 - cx) * near_units
        a = near_units
        col = jnp.where(u < a, mine + low + u,
                        jnp.where(u < units, mine + high + (u - a),
                                  jnp.where(u < units + a, other + low + (u - units), other + high + (u - units - a))))
        return pl.multiple_of(col * LANES, LANES)

    def chunk(s, way):
        return lax.div(s, steps), pl.ds(way * tile, tile), pl.ds(unit_col(lax.rem(s, steps)), LANES)

    def sum_copy(s, way, nxt):
        slot = lax.rem(s, SLOTS)
        return send(yacc.at[chunk(s, way)], rbuf.at[way, slot], rs_send.at[way, slot], rs_recv.at[way, slot], tp=nxt)

    def done_copy(s, way, prv, src):
        slot = lax.rem(s, SLOTS)
        return send(src, yd_ref.at[chunk(s, way)], ag_send.at[way, slot], ag_recv.at[way, slot], tp=prv)

    def tick(tau):
        with jax.named_scope('tick'):
            tick_body(tau)

    def tick_body(tau):
        for way in (0, 1):
            p = t if way == 0 else 3 - t
            nxt = t + 1 if way == 0 else t - 1
            prv = t - 1 if way == 0 else t + 1
            s = tau - p
            slot = lax.rem(jnp.maximum(s, 0), SLOTS)
            live = jnp.logical_and(s >= 0, s < 2 * steps)

            @pl.when(jnp.logical_and(live, p > 0))
            def _():
                wait(rbuf.at[way, slot], rs_recv.at[way, slot])

            @pl.when(jnp.logical_and(live, p < 3))
            def _():
                @pl.when(s >= SLOTS)
                def _():
                    wait(rbuf.at[way, slot], rs_send.at[way, slot])

                @pl.when(p > 0)
                def _():
                    here = chunk(s, way)
                    yacc[here] = yacc[here] + rbuf[way, slot]

                sum_copy(s, way, nxt).start()

            @pl.when(jnp.logical_and(live, p == 3))
            def _():
                @pl.when(s >= SLOTS)
                def _():
                    wait(fin.at[way, slot], ag_send.at[way, slot])
                    wait(fin.at[way, slot], fin_own.at[way, slot])

                here = chunk(s, way)
                fin[way, slot] = (yacc[here] + rbuf[way, slot]).astype(BF16)
                pltpu.make_async_copy(fin.at[way, slot], yd_ref.at[here], fin_own.at[way, slot]).start()
                done_copy(s, way, prv, fin.at[way, slot]).start()

            s2 = tau - 6 + p
            slot2 = lax.rem(jnp.maximum(s2, 0), SLOTS)
            live2 = jnp.logical_and(jnp.logical_and(s2 >= 0, s2 < 2 * steps), p < 3)

            @pl.when(live2)
            def _():
                here = yd_ref.at[chunk(s2, way)]
                wait(here, ag_recv.at[way, slot2])

                @pl.when(p > 0)
                def _():
                    @pl.when(s2 >= SLOTS)
                    def _():
                        wait(fin.at[way, slot2], ag_send.at[way, slot2])

                    done_copy(s2, way, prv, here).start()

    def ticks(lo, hi):
        def body(n, c):
            tick(n)
            return c

        lax.fori_loop(lo, hi, body, 0)

    def drain_sums():
        def body(n, carry):
            for way in (0, 1):
                p = t if way == 0 else 3 - t
                slot = n

                @pl.when(p < 3)
                def _():
                    wait(rbuf.at[way, slot], rs_send.at[way, slot])

                @pl.when(p > 0)
                def _():
                    wait(fin.at[way, slot], ag_send.at[way, slot])

                @pl.when(p == 3)
                def _():
                    wait(fin.at[way, slot], fin_own.at[way, slot])
            return carry

        lax.fori_loop(0, SLOTS, body, 0)

    for ten in (0, 1):
        own_copy(ten).start()
    w_start(0)
    w_start(1)
    base = jnp.where(t == 0, 1.0, 0.0).astype(F32)

    with jax.named_scope('clear'):
        for r in (0, 1):
            for ten in (0, 1):
                load_a(ten, 2 + r)

        def clear(n, carry):
            at = pl.ds(pl.multiple_of(n * 32, 32), 32)
            for k in range(3):
                acc[k, at, :] = jnp.zeros((32, half), F32)
            return carry

        lax.fori_loop(0, win // 32, clear, 0)

        def clear_ab(n, carry):
            lo = pl.ds(pl.multiple_of(n * group, group), group)
            for m in range(4):
                a_all[m, lo, :] = jnp.zeros((group, half), F32)
                b_all[m, lo, :] = jnp.zeros((group, half), F32)
            return carry

        lax.fori_loop(0, tile // group, clear_ab, 0)
        for r in (0, 1):
            for ten in (0, 1):
                loaded(ten, r)

                def residual(n, carry):
                    lo = pl.ds(pl.multiple_of(n * group, group), group)
                    there = pl.ds(pl.multiple_of(r * tile + n * group, group), group)
                    yacc[ten, there, :] = tok_t[ten][r, lo, :].astype(F32) * base
                    return carry

                lax.fori_loop(0, tile // group, residual, 0)
        for ten in (0, 1):
            wait(tok_p[ten], own_recv.at[ten])

    with jax.named_scope('w_relay'):
        w_relay(0)
        w_relay(1)
    w_start(2)

    def ab_pass(last):
        row = cy if last == 0 else 1 - cy
        at_k = pl.ds(pl.multiple_of(row * line, LANES), line)
        load_a(0, 0)

        def body(n, carry):
            slot = lax.rem(n, 2)

            @pl.when(n < 3)
            def _():
                load_a(0, n + 1)

            loaded(0, slot)
            with jax.named_scope('ab_half'):
                x_half = xt[slot, :, at_k]
                a_all[n] += dot_nn(x_half, w_s[0, at_k, :])
                b_all[n] += dot_nn(x_half, w_s[1, at_k, :])

            if last:
                def hidden(m, c):
                    lo = pl.ds(pl.multiple_of(m * group, group), group)
                    a = a_all[n, lo, :]
                    h_all[n, lo, :] = (a * sigmoid(a) * b_all[n, lo, :]).astype(BF16)
                    return c

                lax.fori_loop(0, tile // group, hidden, 0)
            return carry

        lax.fori_loop(0, 4, body, 0)

    with jax.named_scope('w_have'):
        for k in (0, 1):
            w_have(k, 'chip')
            w_have(k, 'x')
    ab_pass(0)
    with jax.named_scope('w_have'):
        for k in (0, 1):
            w_have(k, 'y')
            w_have(k, 'far')
    ab_pass(1)

    def y_group(g):
        u0 = (0, near_units, units, units + near_units)[g]
        n_u = (near_units, rest_units)[g % 2]
        col = unit_col(u0)
        cols = pl.ds(col, n_u * LANES)

        def theirs(r, carry):
            if g > 0:
                before = (near_units, rest_units)[(g - 1) % 2] * LANES
                wait(sb.at[r, :, pl.ds(0, before)], y_send.at[(g - 1) % 2, r])
            with jax.named_scope('y_dot'):
                sb[r, :, :n_u * LANES] = dot_nt(h_all[r], w_s[2, cols, :])
            send(sb.at[r, :, pl.ds(0, n_u * LANES)], pbuf.at[rows_of(r), cols],
                 y_send.at[g % 2, r], y_recv.at[g, r], dp=partner).start()
            return carry

        def ours(r, carry):
            with jax.named_scope('y_wait'):
                wait(pbuf.at[rows_of(r), cols], y_recv.at[g, r])
            with jax.named_scope('y_dot'):
                yacc[0, rows_of(r), cols] = (yacc[0, rows_of(r), cols] + pbuf[rows_of(r), cols]
                                             + dot_nt(h_all[2 + r], w_s[2, cols, :]))
            pl.semaphore_signal(credit, inc=1, device_id={'dp': partner, 'tp': t}, device_id_type=MESH)
            return carry

        lax.fori_loop(0, 2, theirs, 0)
        lax.fori_loop(0, 2, ours, 0)

    with jax.named_scope('w_have2'):
        w_have(2, 'chip')
    y_group(0)
    tick(0)
    with jax.named_scope('w_relay2'):
        w_relay(2)
    q_start(0)
    q_start(1)
    ticks(1, 4)
    with jax.named_scope('w_have2'):
        w_have(2, 'x')
        w_have(2, 'y')
    y_group(1)
    tick(4)
    y_group(2)
    q_start(2)
    ticks(5, 7)
    with jax.named_scope('w_have2'):
        w_have(2, 'far')
    y_group(3)
    q_start(3)
    tick(7)

    first = pl.multiple_of(lax.div(chip * 2 * blk, LANES) * LANES, LANES)
    shift = chip * 2 * blk - first
    at_win = pl.ds(first, win)
    n_block = 3
    n_cols = model // n_block

    def w_grad(k, core):
        return acc.at[k, pl.ds(pl.multiple_of(shift + core * blk, 8), blk), :]

    def put_grad(k):
        send(w_grad(k, 1 - j), outs[k].at[:, w_cols(j)], out_send.at[k], out_recv.at[k], dp=partner).start()
        pltpu.make_async_copy(w_grad(k, j), outs[k].at[:, w_cols(j)], out_own.at[k]).start()

    def dx_tile(n):
        r = lax.rem(n, 2)

        def theirs(m, carry):
            cols = pl.ds(pl.multiple_of(m * n_cols, n_cols), n_cols)
            slot = lax.rem(m + r * n_block, 2)

            @pl.when(m + r * n_block >= 2)
            def _():
                wait(sb.at[slot], dx_send.at[slot])

            with jax.named_scope('dx_dot'):
                sb[slot] = dot_nt(h_all[1], w_s[0, cols, :]) + dot_nt(h_all[2], w_s[1, cols, :])
            send(sb.at[slot], pbuf.at[rows_of(r), cols], dx_send.at[slot], dx_recv.at[r, m], dp=partner).start()
            return carry

        def ours(m, carry):
            cols = pl.ds(pl.multiple_of(m * n_cols, n_cols), n_cols)
            with jax.named_scope('dx_wait'):
                wait(pbuf.at[rows_of(r), cols], dx_recv.at[r, m])
            with jax.named_scope('dx_dot'):
                yacc[1, rows_of(r), cols] = (yacc[1, rows_of(r), cols] + pbuf[rows_of(r), cols]
                                             + (dot_nt(h_all[1], w_s[0, cols, :]) + dot_nt(h_all[2], w_s[1, cols, :])))
            return carry

        @pl.when(n == 0)
        def _():
            pl.semaphore_wait(credit, 8)
            for r_ in (0, 1):
                wait(sb.at[r_, :, pl.ds(0, rest_units * LANES)], y_send.at[1, r_])

        @pl.when(n < 2)
        def _():
            lax.fori_loop(0, n_block, theirs, 0)

        @pl.when(n >= 2)
        def _():
            lax.fori_loop(0, n_block, ours, 0)

    load_a(1, 0)
    load_a(0, 0)

    def grad_tile(n, carry):
        q = n - 4
        slot = lax.rem(n, 2)
        at = jnp.where(n < 4, n, slot)
        final = n == 15

        @pl.when(n < 4)
        def _():
            q_start(4 + n)

        loaded(0, slot)

        @pl.when(n >= 4)
        def _():
            with jax.named_scope('ab'):
                a_all[at] = dot_nn(xt[slot], w_s[0])
                b_all[at] = dot_nn(xt[slot], w_s[1])

            @pl.when(final)
            def _():
                arrive(1, q)

            load_b(1, q)
        tick(jnp.where(n < 4, 8 + 2 * n, jnp.where(q < 6, 16 + 2 * q, 28 + 3 * (q - 6))))
        loaded(1, slot)
        with jax.named_scope('g_dot'):
            g_s[...] = dot_nn(dyt[slot], w_s[2])

        with jax.named_scope('act'):
            def body(m, c):
                lo = pl.ds(pl.multiple_of(m * group, group), group)
                a = a_all[at, lo, :]
                b = b_all[at, lo, :]
                g = g_s[lo, :]
                s = sigmoid(a)
                silu = a * s
                h_all[0, lo, :] = (silu * b).astype(BF16)
                h_all[1, lo, :] = (g * b * s * (1.0 + a * (1.0 - s))).astype(BF16)
                h_all[2, lo, :] = (g * silu).astype(BF16)
                return c

            lax.fori_loop(0, tile // group, body, 0)

        @pl.when(jnp.logical_and(n >= 10, n < 15))
        def _():
            tick(29 + 3 * (q - 6))

        @pl.when(n < 3)
        def _():
            load_a(0, n + 1)
            load_a(1, n + 1)

        @pl.when(jnp.logical_and(n >= 3, n < 15))
        def _():
            arrive(0, q + 1)

        with jax.named_scope('dw_dot'):
            x_win = xt[slot, :, at_win]
            acc[0] += dot_tn(x_win, h_all[1])

            @pl.when(final)
            def _():
                put_grad(0)

            acc[1] += dot_tn(x_win, h_all[2])

            @pl.when(final)
            def _():
                put_grad(1)

            acc[2] += dot_tn(dyt[slot, :, at_win], h_all[0])

            @pl.when(final)
            def _():
                put_grad(2)

        @pl.when(n < 4)
        def _():
            dx_tile(n)

        tick(jnp.where(n < 4, 9 + 2 * n, jnp.where(q < 6, 17 + 2 * q, 30 + 3 * (q - 6))))

        @pl.when(jnp.logical_and(n >= 3, n < 15))
        def _():
            load_b(0, q + 1)

            @pl.when(n < 14)
            def _():
                arrive(1, q + 1)
        return carry

    lax.fori_loop(0, 16, grad_tile, 0)

    with jax.named_scope('drain_sums'):
        drain_sums()
    with jax.named_scope('drain'):
        for slot in (0, 1):
            wait(sb.at[slot], dx_send.at[slot])
        for k in range(3):
            for core in (0, 1):
                for link in (0, 1):
                    for part in (0, 1):
                        w_copy(k, link, part, core).wait_send()
                    w_relay_copy(k, link, core).wait_send()
            w_partner_copy(k).wait_send()
        for ten in (0, 1):
            own_copy(ten).wait_send()

        def drain(q, carry):
            for ten in (0, 1):
                for link in (0, 1):
                    @pl.when(q < 8)
                    def _():
                        wait(slot_of(ten, 0, link, j), q_send.at[lax.rem(q, 8), link, ten])

                    @pl.when(q < 4)
                    def _():
                        wait(slot_of(ten, 0, link, j), rl_send.at[lax.rem(q, 4), link, ten])

                    wait(slot_of(ten, q, link, j), f_send.at[q, link, ten])
            return carry

        lax.fori_loop(0, 12, drain, 0)
    with jax.named_scope('drain_out'):
        for k in range(3):
            wait(w_grad(k, j), out_own.at[k])
            wait(w_grad(k, 1 - j), out_send.at[k])
            wait(w_grad(k, j), out_recv.at[k])


def window(model, blk):
    starts = [(2 * blk * c) // LANES * LANES for c in range(model // (2 * blk))]
    shift = max(2 * blk * c - s for c, s in enumerate(starts))
    return -(-(shift + 2 * blk) // LANES) * LANES


def mlp(x, dy, wg, wu, wd):
    rows, model = x.shape
    blk, width = wg.shape
    half = width // 2
    tile = rows // 2
    dma = pltpu.SemaphoreType.DMA
    vmem = pltpu.VMEM
    anywhere = pl.BlockSpec(memory_space=pl.ANY)
    shape = jax.ShapeDtypeStruct
    flops = 2 * model * half * rows * 2 * 20
    return pl.pallas_call(
        kernel,
        name='mlp',
        out_shape=(shape((2, rows, model), BF16),
                   shape((blk, width), F32), shape((blk, width), F32), shape((blk, width), F32),
                   shape((12, tile, model), BF16), shape((12, tile, model), BF16),
                   shape((rows, model), BF16), shape((rows, model), BF16)),
        in_specs=[anywhere] * 5,
        out_specs=tuple([anywhere] * 8),
        scratch_shapes=[
            vmem((3, model, half), BF16),
            vmem((3, window(model, blk), half), F32),
            vmem((2, rows, model), F32),
            vmem((rows, model), F32),
            vmem((2, tile, model // 3), F32),
            vmem((2, tile, model), BF16),
            vmem((2, tile, model), BF16),
            vmem((4, tile, half), F32),
            vmem((4, tile, half), F32),
            vmem((tile, half), F32),
            vmem((4, tile, half), BF16),
            vmem((2, SLOTS, tile, LANES), F32),
            vmem((2, SLOTS, tile, LANES), BF16),
            dma((3, 2, 2, 2)), dma((3, 2, 2, 2)), dma((3, 2, 2)), dma((3, 2, 2)), dma((3,)), dma((3,)), dma((3,)),
            dma((2,)), dma((2,)), dma((8, 2, 2)), dma((12, 2, 2)), dma((4, 2, 2)), dma((12, 2, 2)), dma((12, 2, 2)),
            dma((2, 2)), dma((4, 2)), dma((2,)), dma((2, 3)), pltpu.SemaphoreType.REGULAR,
            dma((2, SLOTS)), dma((2, SLOTS)), dma((2, SLOTS)), dma((2, SLOTS)), dma((2, SLOTS)),
            dma((2, 2)), dma((3,)), dma((3,)), dma((3,)),
        ],
        compiler_params=pltpu.CompilerParams(collective_id=0, has_side_effects=True, vmem_limit_bytes=67_000_000),
        cost_estimate=pl.CostEstimate(flops=flops, bytes_accessed=100_000_000, transcendentals=0),
    )(x, dy, wg, wu, wd)


def solution(mesh):
    def device_pass(x_rows, gate_blk, up_blk, down_blk, dy_rows):
        out = mlp(x_rows, dy_rows, gate_blk, up_blk, down_blk.T)
        yd, dw_gate, dw_up, dw_down = out[:4]
        return yd[0], yd[1], dw_gate, dw_up, dw_down.T

    row_spec = P('dp', None)
    weight_spec = P('dp', 'tp')
    down_spec = P('tp', 'dp')
    return jax.shard_map(device_pass, mesh=mesh,
                         in_specs=(row_spec, weight_spec, weight_spec, down_spec, row_spec),
                         out_specs=(row_spec, row_spec, weight_spec, weight_spec, down_spec),
                         check_vma=False)
```

time: 384 us -> 366 us (0.953)
  Pallas kernels: 371 us -> 353 us
    pallas_call x1, Pallas kernels: 371 us -> 353 us  [mlp(): pl.pallas_call(kernel, name='mlp', out_shape=(shape((2, rows, model), BF1...]
where the time goes in v3:
time: 366 us; the launch traced here: 365 us
  Pallas kernels  353 us (96%)
  local copies, waits for them, and re-layouts  11.9 us (3%)
    pallas_call x1, Pallas kernels, mlp(): pl.pallas_call(kernel, name='mlp', out_shape=(shape((2, rows, model), BF1...  353 us

profile of v3, /device:TPU:0, one launch (start us, length us, event | category | flops | bytes accessed | tf_op | source)
XLA Modules:
  0.0 365.4 jit_solution(5566193860870863416)
XLA Ops:
  0.6 352.8 %mlp.1 = (bf16[2,512,2304]{2,1,0:T(8,128)(2,1)}, f32[288,2304]{1,0:T(8,128)}, f32[288,2304]{1,0:T(8,128)}, f32[288,2304]{1,0:T(8,128)}, bf16[12,256,2304]{2,1,0:...) custom-call(bf16[512,2304]{1,0:T(8,128)(2,1)} %x_ref.1, ...), custom_call_target="tpu_custom_call" | custom-call | flops 108716359680 | bytes 100000000 | tf_op jit(solution)/shard_map/mlp/pallas_call | solution.py:657
  353.4 0.0 copy-start.2
  353.5 5.0 %slice_bitcast_fusion = (bf16[512,2304]{1,0:T(8,128)(2,1)}, bf16[512,2304]{1,0:T(8,128)(2,1)}) fusion(bf16[2,512,2304]{2,1,0:T(8,128)(2,1)} %get-tuple-element.9), kind=kLoop, calls=%fused_computation | loop fusion | bytes 9437184 | tf_op jit(solution)/shard_map/squeeze | solution.py:695
  358.5 0.0 copy-done.2
  358.5 0.0 copy-start.1
  358.5 1.5 copy.13
  360.0 1.2 copy-done.1
  361.2 0.0 copy-start
  361.2 1.5 copy.14
  362.7 1.2 copy-done
  363.9 1.5 copy.15
Async XLA Ops:
  353.4 5.0 %copy-start.2 = (f32[288,2304]{1,0:T(8,128)S(1)}, f32[288,2304]{1,0:T(8,128)}, u32[]{:S(2)}) copy-start(f32[288,2304]{1,0:T(8,128)} %get-tuple-element.22) | copy-start | bytes 7962628
  358.5 2.7 copy-start.1
  361.2 2.7 copy-start
